TPU v7x, 8 devices: a whole 2x2x1 slice. The times are simulated.
8 devices in a mesh: task: 1 (over z), row: 8 (over y, x, core).
Axes of the slice: x: 2, y: 2, z: 1, core: 2. Of those that a mesh axis runs over, the one named last changes fastest.
Arguments:
- points: bfloat16 [24576, 512], P(('task', 'row'))
- vectors: bfloat16 [24576, 64], P(('task', 'row'))
- length_scale: float32 [1], P('task')
- out_scale: float32 [1], P('task')
Outputs:
- output: float32 [24576, 64], P(('task', 'row'))
All inputs are finite; a program needn't handle non-finite values.
Results may differ from a plain program's by a relative error of at most 0.001.
Values are sent between devices in bfloat16 or wider.
A program may use at most 1 GiB of HBM per device.

v0:
```python
import jax
import jax.numpy as jnp
from jax import lax
from jax.sharding import PartitionSpec as P


def solution(mesh):
    n_row = mesh.shape["row"]
    shift_pairs = [(source_idx, (source_idx + 1) % n_row) for source_idx in range(n_row)]

    def kernel_product(x_rows, norm_rows, x_cols, norm_cols, v_cols, length_scale, out_scale):
        gram_mat = jnp.einsum("if,jf->ij", x_rows, x_cols, preferred_element_type=jnp.float32)
        sq_dist = jnp.maximum(norm_rows[:, None] + norm_cols[None, :] - 2.0 * gram_mat, 0.0)
        kern_tile = (out_scale * jnp.exp(-sq_dist / (2.0 * length_scale * length_scale))).astype(jnp.bfloat16)
        return jnp.dot(kern_tile, v_cols, preferred_element_type=jnp.float32)

    def kernel_pass(x_loc, norm_loc, v_loc, length_scale, out_scale):
        own_part = kernel_product(x_loc, norm_loc, x_loc, norm_loc, v_loc, length_scale, out_scale)

        def visit_step(step_idx, loop_state):
            x_vis, v_vis, running = loop_state
            x_vis = lax.ppermute(x_vis, "row", shift_pairs)
            v_vis = lax.ppermute(v_vis, "row", shift_pairs)
            norm_vis = jnp.sum(jnp.square(x_vis.astype(jnp.float32)), axis=1)
            running = running + kernel_product(x_loc, norm_loc, x_vis, norm_vis, v_vis, length_scale, out_scale)
            return x_vis, v_vis, running

        final_state = lax.fori_loop(1, n_row, visit_step, (x_loc, v_loc, own_part))
        return final_state[2]

    def local_program(x_loc, v_loc, length_scale, out_scale):
        norm_loc = jnp.sum(jnp.square(x_loc.astype(jnp.float32)), axis=1)
        first_pass = kernel_pass(x_loc, norm_loc, v_loc, length_scale, out_scale).astype(jnp.bfloat16)
        return kernel_pass(x_loc, norm_loc, first_pass, length_scale, out_scale)

    row_spec = P(("task", "row"), None)
    return jax.shard_map(local_program, mesh=mesh, in_specs=(row_spec, row_spec, P("task"), P("task")), out_specs=row_spec, check_vma=False)
```

profile of v0, /device:TPU:0, one launch (start us, length us, event | category | flops | bytes accessed | tf_op | source)
XLA Modules:
  0.0 993.2 jit_solution(6704231883763845580)
XLA Ops:
  0.0 1.8 copy.34
  2.4 3.2 multiply_reduce_fusion.2
  6.3 17.6 %multiply_convert_fusion.2 = bf16[3072,3072]{1,0:T(8,128)(2,1)S(1)} fusion(bf16[3072,512]{1,0:T(8,128)(2,1)} %param.8, f32[]{:T(128)} %bitcast.5, f32[3072]{0:T(1024)} %multiply_reduce_fusion.2, f32[]{:T(128)} %bitcast.38), kind=kOutput, calls=%fused_computation.10 | convolution fusion | flops 9739173888 | bytes 22032392 | tf_op jit(solution)/shard_map/if,jf->ij/dot_general | solution.py:12
  23.9 6.5 copy-done
  30.4 7.7 fusion.4
  38.0 3.8 copy.7
  41.8 468.2 %while.32 = (s32[]{:T(128)}, bf16[3072,512]{1,0:T(8,128)(2,1)}, bf16[3072,64]{0,1:T(8,128)(2,1)}, f32[3072,64]{0,1:T(8,128)}, f32[1]{0:T(128)}, /*index=5*/f32[3...) while((s32[]{:T(128)}, bf16[3072,512]{1,0:T(8,128)(2,1)}, bf16[3072,64]{0,1:T(8,128)(2,1)}, ...), condition=%wide.region_3.0_spmd, body=%wide.region_1.0_spmd.sunk | while | flops 10952045568 | bytes 32673972 | solution.py:28
  41.8 0.9 collective-permute-start
  42.7 2.6 collective-permute-start.1
  45.3 39.5 %collective-permute-done.1 = bf16[3072,64]{0,1:T(8,128)(2,1)S(1)} collective-permute-done((bf16[3072,64]{0,1:T(8,128)(2,1)}, bf16[3072,64]{0,1:T(8,128)(2,1)S(1)}, u32[]{:S(2)}, u32[]{:S(2)}) %collective-permute-start.1) | collective-permute-done | bytes 393248 | tf_op jit(solution)/shard_map/while/body/eval_jaxpr/ppermute | solution.py:23
  84.7 0.8 copy.16
  86.2 1.7 copy.15
  87.9 21.8 %convolution_add_fusion.4 = f32[3072,64]{0,1:T(8,128)} fusion(f32[3072,64]{0,1:T(8,128)} %get-tuple-element.339, bf16[3072,64]{0,1:T(8,128)(2,1)S(1)} %collective-permute-done.1, bf16[3072,512]{1,0:T(8,128)(2,1)} %get-tuple-element.351, bf16[3072,512]{1,0:T(8,128)(2,1)S(1)} %collective-permute-done, f32[]{:T(128)} %bitcast.31, ...), kind=kOutput, calls=%fused_computation.2.clone.1 | convolution fusion | flops 10947330048 | bytes 8282120 | tf_op jit(solution)/shard_map/while/body/eval_jaxpr/dot_general | solution.py:15
  109.6 1.5 collective-permute-start.1
  111.1 40.3 %collective-permute-done.1 = bf16[3072,64]{0,1:T(8,128)(2,1)S(1)} collective-permute-done((bf16[3072,64]{0,1:T(8,128)(2,1)}, bf16[3072,64]{0,1:T(8,128)(2,1)S(1)}, u32[]{:S(2)}, u32[]{:S(2)}) %collective-permute-start.1) | collective-permute-done | bytes 393248 | tf_op jit(solution)/shard_map/while/body/eval_jaxpr/ppermute | solution.py:23
  151.4 0.8 copy.16
  152.9 1.7 copy.15
  154.6 21.8 %convolution_add_fusion.4 = f32[3072,64]{0,1:T(8,128)} fusion(f32[3072,64]{0,1:T(8,128)} %get-tuple-element.339, bf16[3072,64]{0,1:T(8,128)(2,1)S(1)} %collective-permute-done.1, bf16[3072,512]{1,0:T(8,128)(2,1)} %get-tuple-element.351, bf16[3072,512]{1,0:T(8,128)(2,1)S(1)} %collective-permute-done, f32[]{:T(128)} %bitcast.31, ...), kind=kOutput, calls=%fused_computation.2.clone.1 | convolution fusion | flops 10947330048 | bytes 8282120 | tf_op jit(solution)/shard_map/while/body/eval_jaxpr/dot_general | solution.py:15
  177.0 41.2 %collective-permute-done.1 = bf16[3072,64]{0,1:T(8,128)(2,1)S(1)} collective-permute-done((bf16[3072,64]{0,1:T(8,128)(2,1)}, bf16[3072,64]{0,1:T(8,128)(2,1)S(1)}, u32[]{:S(2)}, u32[]{:S(2)}) %collective-permute-start.1) | collective-permute-done | bytes 393248 | tf_op jit(solution)/shard_map/while/body/eval_jaxpr/ppermute | solution.py:23
  218.2 0.8 copy.16
  219.6 1.7 copy.15
  221.3 21.8 %convolution_add_fusion.4 = f32[3072,64]{0,1:T(8,128)} fusion(f32[3072,64]{0,1:T(8,128)} %get-tuple-element.339, bf16[3072,64]{0,1:T(8,128)(2,1)S(1)} %collective-permute-done.1, bf16[3072,512]{1,0:T(8,128)(2,1)} %get-tuple-element.351, bf16[3072,512]{1,0:T(8,128)(2,1)S(1)} %collective-permute-done, f32[]{:T(128)} %bitcast.31, ...), kind=kOutput, calls=%fused_computation.2.clone.1 | convolution fusion | flops 10947330048 | bytes 8282120 | tf_op jit(solution)/shard_map/while/body/eval_jaxpr/dot_general | solution.py:15
  243.1 41.8 %collective-permute-done.1 = bf16[3072,64]{0,1:T(8,128)(2,1)S(1)} collective-permute-done((bf16[3072,64]{0,1:T(8,128)(2,1)}, bf16[3072,64]{0,1:T(8,128)(2,1)S(1)}, u32[]{:S(2)}, u32[]{:S(2)}) %collective-permute-start.1) | collective-permute-done | bytes 393248 | tf_op jit(solution)/shard_map/while/body/eval_jaxpr/ppermute | solution.py:23
  284.9 0.8 copy.16
  286.4 1.7 copy.15
  288.1 21.8 %convolution_add_fusion.4 = f32[3072,64]{0,1:T(8,128)} fusion(f32[3072,64]{0,1:T(8,128)} %get-tuple-element.339, bf16[3072,64]{0,1:T(8,128)(2,1)S(1)} %collective-permute-done.1, bf16[3072,512]{1,0:T(8,128)(2,1)} %get-tuple-element.351, bf16[3072,512]{1,0:T(8,128)(2,1)S(1)} %collective-permute-done, f32[]{:T(128)} %bitcast.31, ...), kind=kOutput, calls=%fused_computation.2.clone.1 | convolution fusion | flops 10947330048 | bytes 8282120 | tf_op jit(solution)/shard_map/while/body/eval_jaxpr/dot_general | solution.py:15
  309.8 41.8 %collective-permute-done.1 = bf16[3072,64]{0,1:T(8,128)(2,1)S(1)} collective-permute-done((bf16[3072,64]{0,1:T(8,128)(2,1)}, bf16[3072,64]{0,1:T(8,128)(2,1)S(1)}, u32[]{:S(2)}, u32[]{:S(2)}) %collective-permute-start.1) | collective-permute-done | bytes 393248 | tf_op jit(solution)/shard_map/while/body/eval_jaxpr/ppermute | solution.py:23
  351.6 0.8 copy.16
  353.1 1.7 copy.15
  354.8 21.8 %convolution_add_fusion.4 = f32[3072,64]{0,1:T(8,128)} fusion(f32[3072,64]{0,1:T(8,128)} %get-tuple-element.339, bf16[3072,64]{0,1:T(8,128)(2,1)S(1)} %collective-permute-done.1, bf16[3072,512]{1,0:T(8,128)(2,1)} %get-tuple-element.351, bf16[3072,512]{1,0:T(8,128)(2,1)S(1)} %collective-permute-done, f32[]{:T(128)} %bitcast.31, ...), kind=kOutput, calls=%fused_computation.2.clone.1 | convolution fusion | flops 10947330048 | bytes 8282120 | tf_op jit(solution)/shard_map/while/body/eval_jaxpr/dot_general | solution.py:15
  376.6 41.8 %collective-permute-done.1 = bf16[3072,64]{0,1:T(8,128)(2,1)S(1)} collective-permute-done((bf16[3072,64]{0,1:T(8,128)(2,1)}, bf16[3072,64]{0,1:T(8,128)(2,1)S(1)}, u32[]{:S(2)}, u32[]{:S(2)}) %collective-permute-start.1) | collective-permute-done | bytes 393248 | tf_op jit(solution)/shard_map/while/body/eval_jaxpr/ppermute | solution.py:23
  418.4 0.8 copy.16
  419.8 1.7 copy.15
  421.5 21.8 %convolution_add_fusion.4 = f32[3072,64]{0,1:T(8,128)} fusion(f32[3072,64]{0,1:T(8,128)} %get-tuple-element.339, bf16[3072,64]{0,1:T(8,128)(2,1)S(1)} %collective-permute-done.1, bf16[3072,512]{1,0:T(8,128)(2,1)} %get-tuple-element.351, bf16[3072,512]{1,0:T(8,128)(2,1)S(1)} %collective-permute-done, f32[]{:T(128)} %bitcast.31, ...), kind=kOutput, calls=%fused_computation.2.clone.1 | convolution fusion | flops 10947330048 | bytes 8282120 | tf_op jit(solution)/shard_map/while/body/eval_jaxpr/dot_general | solution.py:15
  443.3 41.8 %collective-permute-done.1 = bf16[3072,64]{0,1:T(8,128)(2,1)S(1)} collective-permute-done((bf16[3072,64]{0,1:T(8,128)(2,1)}, bf16[3072,64]{0,1:T(8,128)(2,1)S(1)}, u32[]{:S(2)}, u32[]{:S(2)}) %collective-permute-start.1) | collective-permute-done | bytes 393248 | tf_op jit(solution)/shard_map/while/body/eval_jaxpr/ppermute | solution.py:23
  485.1 0.8 copy.16
  486.6 1.7 copy.15
  488.3 21.8 %convolution_add_fusion.4 = f32[3072,64]{0,1:T(8,128)} fusion(f32[3072,64]{0,1:T(8,128)} %get-tuple-element.339, bf16[3072,64]{0,1:T(8,128)(2,1)S(1)} %collective-permute-done.1, bf16[3072,512]{1,0:T(8,128)(2,1)} %get-tuple-element.351, bf16[3072,512]{1,0:T(8,128)(2,1)S(1)} %collective-permute-done, f32[]{:T(128)} %bitcast.31, ...), kind=kOutput, calls=%fused_computation.2.clone.1 | convolution fusion | flops 10947330048 | bytes 8282120 | tf_op jit(solution)/shard_map/while/body/eval_jaxpr/dot_general | solution.py:15
  510.1 1.3 convert_element_type.32
  511.4 13.2 %fusion.5 = f32[3072,64]{0,1:T(8,128)} fusion(bf16[3072,3072]{1,0:T(8,128)(2,1)} %copy-done, bf16[3072,64]{0,1:T(8,128)(2,1)S(1)} %convert_element_type.32), kind=kOutput, calls=%fused_computation.13 | convolution fusion | flops 1207959552 | bytes 20054016 | tf_op jit(solution)/shard_map/dot_general | solution.py:15
  524.6 1.7 copy.19
  526.3 466.9 %while.33 = (s32[]{:T(128)}, bf16[3072,512]{1,0:T(8,128)(2,1)}, bf16[3072,64]{0,1:T(8,128)(2,1)}, f32[3072,64]{0,1:T(8,128)}, f32[1]{0:T(128)}, /*index=5*/f32[3...) while((s32[]{:T(128)}, bf16[3072,512]{1,0:T(8,128)(2,1)}, bf16[3072,64]{0,1:T(8,128)(2,1)}, ...), condition=%wide.region_6.0_spmd, body=%wide.region_4.0_spmd.sunk | while | flops 10952045568 | bytes 32673972 | solution.py:28
  526.3 41.8 %collective-permute-done.3 = bf16[3072,64]{0,1:T(8,128)(2,1)S(1)} collective-permute-done((bf16[3072,64]{0,1:T(8,128)(2,1)}, bf16[3072,64]{0,1:T(8,128)(2,1)S(1)}, u32[]{:S(2)}, u32[]{:S(2)}) %collective-permute-start.3) | collective-permute-done | bytes 393248 | tf_op jit(solution)/shard_map/while/body/eval_jaxpr/ppermute | solution.py:23
  568.1 0.7 copy.28
  569.5 1.7 copy.27
  571.2 21.8 %convolution_add_fusion.5 = f32[3072,64]{0,1:T(8,128)} fusion(f32[3072,64]{0,1:T(8,128)} %get-tuple-element.366, bf16[3072,64]{0,1:T(8,128)(2,1)S(1)} %collective-permute-done.3, bf16[3072,512]{1,0:T(8,128)(2,1)} %get-tuple-element.378, bf16[3072,512]{1,0:T(8,128)(2,1)S(1)} %collective-permute-done.2, f32[]{:T(128)} %bitcast.36, ...), kind=kOutput, calls=%fused_computation.7.clone.1 | convolution fusion | flops 10947330048 | bytes 8282120 | tf_op jit(solution)/shard_map/while/body/eval_jaxpr/dot_general | solution.py:15
  593.0 41.8 %collective-permute-done.3 = bf16[3072,64]{0,1:T(8,128)(2,1)S(1)} collective-permute-done((bf16[3072,64]{0,1:T(8,128)(2,1)}, bf16[3072,64]{0,1:T(8,128)(2,1)S(1)}, u32[]{:S(2)}, u32[]{:S(2)}) %collective-permute-start.3) | collective-permute-done | bytes 393248 | tf_op jit(solution)/shard_map/while/body/eval_jaxpr/ppermute | solution.py:23
  636.2 1.7 copy.27
  637.9 21.8 %convolution_add_fusion.5 = f32[3072,64]{0,1:T(8,128)} fusion(f32[3072,64]{0,1:T(8,128)} %get-tuple-element.366, bf16[3072,64]{0,1:T(8,128)(2,1)S(1)} %collective-permute-done.3, bf16[3072,512]{1,0:T(8,128)(2,1)} %get-tuple-element.378, bf16[3072,512]{1,0:T(8,128)(2,1)S(1)} %collective-permute-done.2, f32[]{:T(128)} %bitcast.36, ...), kind=kOutput, calls=%fused_computation.7.clone.1 | convolution fusion | flops 10947330048 | bytes 8282120 | tf_op jit(solution)/shard_map/while/body/eval_jaxpr/dot_general | solution.py:15
  659.7 41.8 %collective-permute-done.3 = bf16[3072,64]{0,1:T(8,128)(2,1)S(1)} collective-permute-done((bf16[3072,64]{0,1:T(8,128)(2,1)}, bf16[3072,64]{0,1:T(8,128)(2,1)S(1)}, u32[]{:S(2)}, u32[]{:S(2)}) %collective-permute-start.3) | collective-permute-done | bytes 393248 | tf_op jit(solution)/shard_map/while/body/eval_jaxpr/ppermute | solution.py:23
  702.9 1.7 copy.27
  704.6 21.8 %convolution_add_fusion.5 = f32[3072,64]{0,1:T(8,128)} fusion(f32[3072,64]{0,1:T(8,128)} %get-tuple-element.366, bf16[3072,64]{0,1:T(8,128)(2,1)S(1)} %collective-permute-done.3, bf16[3072,512]{1,0:T(8,128)(2,1)} %get-tuple-element.378, bf16[3072,512]{1,0:T(8,128)(2,1)S(1)} %collective-permute-done.2, f32[]{:T(128)} %bitcast.36, ...), kind=kOutput, calls=%fused_computation.7.clone.1 | convolution fusion | flops 10947330048 | bytes 8282120 | tf_op jit(solution)/shard_map/while/body/eval_jaxpr/dot_general | solution.py:15
  726.4 41.8 %collective-permute-done.3 = bf16[3072,64]{0,1:T(8,128)(2,1)S(1)} collective-permute-done((bf16[3072,64]{0,1:T(8,128)(2,1)}, bf16[3072,64]{0,1:T(8,128)(2,1)S(1)}, u32[]{:S(2)}, u32[]{:S(2)}) %collective-permute-start.3) | collective-permute-done | bytes 393248 | tf_op jit(solution)/shard_map/while/body/eval_jaxpr/ppermute | solution.py:23
  769.6 1.7 copy.27
  771.3 21.8 %convolution_add_fusion.5 = f32[3072,64]{0,1:T(8,128)} fusion(f32[3072,64]{0,1:T(8,128)} %get-tuple-element.366, bf16[3072,64]{0,1:T(8,128)(2,1)S(1)} %collective-permute-done.3, bf16[3072,512]{1,0:T(8,128)(2,1)} %get-tuple-element.378, bf16[3072,512]{1,0:T(8,128)(2,1)S(1)} %collective-permute-done.2, f32[]{:T(128)} %bitcast.36, ...), kind=kOutput, calls=%fused_computation.7.clone.1 | convolution fusion | flops 10947330048 | bytes 8282120 | tf_op jit(solution)/shard_map/while/body/eval_jaxpr/dot_general | solution.py:15
  793.1 41.8 %collective-permute-done.3 = bf16[3072,64]{0,1:T(8,128)(2,1)S(1)} collective-permute-done((bf16[3072,64]{0,1:T(8,128)(2,1)}, bf16[3072,64]{0,1:T(8,128)(2,1)S(1)}, u32[]{:S(2)}, u32[]{:S(2)}) %collective-permute-start.3) | collective-permute-done | bytes 393248 | tf_op jit(solution)/shard_map/while/body/eval_jaxpr/ppermute | solution.py:23
  836.3 1.7 copy.27
  838.0 21.8 %convolution_add_fusion.5 = f32[3072,64]{0,1:T(8,128)} fusion(f32[3072,64]{0,1:T(8,128)} %get-tuple-element.366, bf16[3072,64]{0,1:T(8,128)(2,1)S(1)} %collective-permute-done.3, bf16[3072,512]{1,0:T(8,128)(2,1)} %get-tuple-element.378, bf16[3072,512]{1,0:T(8,128)(2,1)S(1)} %collective-permute-done.2, f32[]{:T(128)} %bitcast.36, ...), kind=kOutput, calls=%fused_computation.7.clone.1 | convolution fusion | flops 10947330048 | bytes 8282120 | tf_op jit(solution)/shard_map/while/body/eval_jaxpr/dot_general | solution.py:15
  859.8 41.8 %collective-permute-done.3 = bf16[3072,64]{0,1:T(8,128)(2,1)S(1)} collective-permute-done((bf16[3072,64]{0,1:T(8,128)(2,1)}, bf16[3072,64]{0,1:T(8,128)(2,1)S(1)}, u32[]{:S(2)}, u32[]{:S(2)}) %collective-permute-start.3) | collective-permute-done | bytes 393248 | tf_op jit(solution)/shard_map/while/body/eval_jaxpr/ppermute | solution.py:23
  903.0 1.7 copy.27
  904.7 21.8 %convolution_add_fusion.5 = f32[3072,64]{0,1:T(8,128)} fusion(f32[3072,64]{0,1:T(8,128)} %get-tuple-element.366, bf16[3072,64]{0,1:T(8,128)(2,1)S(1)} %collective-permute-done.3, bf16[3072,512]{1,0:T(8,128)(2,1)} %get-tuple-element.378, bf16[3072,512]{1,0:T(8,128)(2,1)S(1)} %collective-permute-done.2, f32[]{:T(128)} %bitcast.36, ...), kind=kOutput, calls=%fused_computation.7.clone.1 | convolution fusion | flops 10947330048 | bytes 8282120 | tf_op jit(solution)/shard_map/while/body/eval_jaxpr/dot_general | solution.py:15
  926.5 41.8 %collective-permute-done.3 = bf16[3072,64]{0,1:T(8,128)(2,1)S(1)} collective-permute-done((bf16[3072,64]{0,1:T(8,128)(2,1)}, bf16[3072,64]{0,1:T(8,128)(2,1)S(1)}, u32[]{:S(2)}, u32[]{:S(2)}) %collective-permute-start.3) | collective-permute-done | bytes 393248 | tf_op jit(solution)/shard_map/while/body/eval_jaxpr/ppermute | solution.py:23
  969.7 1.7 copy.27
  971.4 21.8 %convolution_add_fusion.5 = f32[3072,64]{0,1:T(8,128)} fusion(f32[3072,64]{0,1:T(8,128)} %get-tuple-element.366, bf16[3072,64]{0,1:T(8,128)(2,1)S(1)} %collective-permute-done.3, bf16[3072,512]{1,0:T(8,128)(2,1)} %get-tuple-element.378, bf16[3072,512]{1,0:T(8,128)(2,1)S(1)} %collective-permute-done.2, f32[]{:T(128)} %bitcast.36, ...), kind=kOutput, calls=%fused_computation.7.clone.1 | convolution fusion | flops 10947330048 | bytes 8282120 | tf_op jit(solution)/shard_map/while/body/eval_jaxpr/dot_general | solution.py:15
  (64 shorter events, 14.8 us)
Async XLA Ops:
  23.9 6.5 copy-start
  41.8 43.7 %collective-permute-start = (bf16[3072,512]{1,0:T(8,128)(2,1)}, bf16[3072,512]{1,0:T(8,128)(2,1)S(1)}, u32[]{:S(2)}, u32[]{:S(2)}) collective-permute-start(bf16[3072,512]{1,0:T(8,128)(2,1)} %get-tuple-element.337), channel_id=1, source_target_pairs={{0,1},{1,2},{2,3},{3,4},{4,5},{5,6},{6,7},{7,0}} | collective-permute-start | bytes 9437192 | tf_op jit(solution)/shard_map/while/body/eval_jaxpr/ppermute | solution.py:22
  42.7 42.0 %collective-permute-start.1 = (bf16[3072,64]{0,1:T(8,128)(2,1)}, bf16[3072,64]{0,1:T(8,128)(2,1)S(1)}, u32[]{:S(2)}, u32[]{:S(2)}) collective-permute-start(bf16[3072,64]{0,1:T(8,128)(2,1)} %get-tuple-element.338), channel_id=1, source_target_pairs={{0,1},{1,2},{2,3},{3,4},{4,5},{5,6},{6,7},{7,0}} | collective-permute-start | bytes 1179656 | tf_op jit(solution)/shard_map/while/body/eval_jaxpr/ppermute | solution.py:23
  109.6 42.6 %collective-permute-start = (bf16[3072,512]{1,0:T(8,128)(2,1)}, bf16[3072,512]{1,0:T(8,128)(2,1)S(1)}, u32[]{:S(2)}, u32[]{:S(2)}) collective-permute-start(bf16[3072,512]{1,0:T(8,128)(2,1)} %get-tuple-element.337), channel_id=1, source_target_pairs={{0,1},{1,2},{2,3},{3,4},{4,5},{5,6},{6,7},{7,0}} | collective-permute-start | bytes 9437192 | tf_op jit(solution)/shard_map/while/body/eval_jaxpr/ppermute | solution.py:22
  109.6 41.8 %collective-permute-start.1 = (bf16[3072,64]{0,1:T(8,128)(2,1)}, bf16[3072,64]{0,1:T(8,128)(2,1)S(1)}, u32[]{:S(2)}, u32[]{:S(2)}) collective-permute-start(bf16[3072,64]{0,1:T(8,128)(2,1)} %get-tuple-element.338), channel_id=1, source_target_pairs={{0,1},{1,2},{2,3},{3,4},{4,5},{5,6},{6,7},{7,0}} | collective-permute-start | bytes 1179656 | tf_op jit(solution)/shard_map/while/body/eval_jaxpr/ppermute | solution.py:23
  176.4 42.6 %collective-permute-start = (bf16[3072,512]{1,0:T(8,128)(2,1)}, bf16[3072,512]{1,0:T(8,128)(2,1)S(1)}, u32[]{:S(2)}, u32[]{:S(2)}) collective-permute-start(bf16[3072,512]{1,0:T(8,128)(2,1)} %get-tuple-element.337), channel_id=1, source_target_pairs={{0,1},{1,2},{2,3},{3,4},{4,5},{5,6},{6,7},{7,0}} | collective-permute-start | bytes 9437192 | tf_op jit(solution)/shard_map/while/body/eval_jaxpr/ppermute | solution.py:22
  176.4 41.8 %collective-permute-start.1 = (bf16[3072,64]{0,1:T(8,128)(2,1)}, bf16[3072,64]{0,1:T(8,128)(2,1)S(1)}, u32[]{:S(2)}, u32[]{:S(2)}) collective-permute-start(bf16[3072,64]{0,1:T(8,128)(2,1)} %get-tuple-element.338), channel_id=1, source_target_pairs={{0,1},{1,2},{2,3},{3,4},{4,5},{5,6},{6,7},{7,0}} | collective-permute-start | bytes 1179656 | tf_op jit(solution)/shard_map/while/body/eval_jaxpr/ppermute | solution.py:23
  243.1 42.6 %collective-permute-start = (bf16[3072,512]{1,0:T(8,128)(2,1)}, bf16[3072,512]{1,0:T(8,128)(2,1)S(1)}, u32[]{:S(2)}, u32[]{:S(2)}) collective-permute-start(bf16[3072,512]{1,0:T(8,128)(2,1)} %get-tuple-element.337), channel_id=1, source_target_pairs={{0,1},{1,2},{2,3},{3,4},{4,5},{5,6},{6,7},{7,0}} | collective-permute-start | bytes 9437192 | tf_op jit(solution)/shard_map/while/body/eval_jaxpr/ppermute | solution.py:22
  243.1 41.8 %collective-permute-start.1 = (bf16[3072,64]{0,1:T(8,128)(2,1)}, bf16[3072,64]{0,1:T(8,128)(2,1)S(1)}, u32[]{:S(2)}, u32[]{:S(2)}) collective-permute-start(bf16[3072,64]{0,1:T(8,128)(2,1)} %get-tuple-element.338), channel_id=1, source_target_pairs={{0,1},{1,2},{2,3},{3,4},{4,5},{5,6},{6,7},{7,0}} | collective-permute-start | bytes 1179656 | tf_op jit(solution)/shard_map/while/body/eval_jaxpr/ppermute | solution.py:23
  309.8 42.6 %collective-permute-start = (bf16[3072,512]{1,0:T(8,128)(2,1)}, bf16[3072,512]{1,0:T(8,128)(2,1)S(1)}, u32[]{:S(2)}, u32[]{:S(2)}) collective-permute-start(bf16[3072,512]{1,0:T(8,128)(2,1)} %get-tuple-element.337), channel_id=1, source_target_pairs={{0,1},{1,2},{2,3},{3,4},{4,5},{5,6},{6,7},{7,0}} | collective-permute-start | bytes 9437192 | tf_op jit(solution)/shard_map/while/body/eval_jaxpr/ppermute | solution.py:22
  309.8 41.8 %collective-permute-start.1 = (bf16[3072,64]{0,1:T(8,128)(2,1)}, bf16[3072,64]{0,1:T(8,128)(2,1)S(1)}, u32[]{:S(2)}, u32[]{:S(2)}) collective-permute-start(bf16[3072,64]{0,1:T(8,128)(2,1)} %get-tuple-element.338), channel_id=1, source_target_pairs={{0,1},{1,2},{2,3},{3,4},{4,5},{5,6},{6,7},{7,0}} | collective-permute-start | bytes 1179656 | tf_op jit(solution)/shard_map/while/body/eval_jaxpr/ppermute | solution.py:23
  376.6 42.6 %collective-permute-start = (bf16[3072,512]{1,0:T(8,128)(2,1)}, bf16[3072,512]{1,0:T(8,128)(2,1)S(1)}, u32[]{:S(2)}, u32[]{:S(2)}) collective-permute-start(bf16[3072,512]{1,0:T(8,128)(2,1)} %get-tuple-element.337), channel_id=1, source_target_pairs={{0,1},{1,2},{2,3},{3,4},{4,5},{5,6},{6,7},{7,0}} | collective-permute-start | bytes 9437192 | tf_op jit(solution)/shard_map/while/body/eval_jaxpr/ppermute | solution.py:22
  376.6 41.8 %collective-permute-start.1 = (bf16[3072,64]{0,1:T(8,128)(2,1)}, bf16[3072,64]{0,1:T(8,128)(2,1)S(1)}, u32[]{:S(2)}, u32[]{:S(2)}) collective-permute-start(bf16[3072,64]{0,1:T(8,128)(2,1)} %get-tuple-element.338), channel_id=1, source_target_pairs={{0,1},{1,2},{2,3},{3,4},{4,5},{5,6},{6,7},{7,0}} | collective-permute-start | bytes 1179656 | tf_op jit(solution)/shard_map/while/body/eval_jaxpr/ppermute | solution.py:23
  443.3 42.6 %collective-permute-start = (bf16[3072,512]{1,0:T(8,128)(2,1)}, bf16[3072,512]{1,0:T(8,128)(2,1)S(1)}, u32[]{:S(2)}, u32[]{:S(2)}) collective-permute-start(bf16[3072,512]{1,0:T(8,128)(2,1)} %get-tuple-element.337), channel_id=1, source_target_pairs={{0,1},{1,2},{2,3},{3,4},{4,5},{5,6},{6,7},{7,0}} | collective-permute-start | bytes 9437192 | tf_op jit(solution)/shard_map/while/body/eval_jaxpr/ppermute | solution.py:22
  443.3 41.8 %collective-permute-start.1 = (bf16[3072,64]{0,1:T(8,128)(2,1)}, bf16[3072,64]{0,1:T(8,128)(2,1)S(1)}, u32[]{:S(2)}, u32[]{:S(2)}) collective-permute-start(bf16[3072,64]{0,1:T(8,128)(2,1)} %get-tuple-element.338), channel_id=1, source_target_pairs={{0,1},{1,2},{2,3},{3,4},{4,5},{5,6},{6,7},{7,0}} | collective-permute-start | bytes 1179656 | tf_op jit(solution)/shard_map/while/body/eval_jaxpr/ppermute | solution.py:23
  510.0 14.5 %copy-start.1 = (bf16[3072,512]{1,0:T(8,128)(2,1)S(1)}, bf16[3072,512]{1,0:T(8,128)(2,1)}, u32[]{:S(2)}) copy-start(bf16[3072,512]{1,0:T(8,128)(2,1)} %get-tuple-element.383) | copy-start | bytes 9437188
  511.4 14.9 %copy-start.2 = (bf16[3072,64]{0,1:T(8,128)(2,1)}, bf16[3072,64]{0,1:T(8,128)(2,1)S(1)}, u32[]{:S(2)}) copy-start(bf16[3072,64]{0,1:T(8,128)(2,1)S(1)} %convert_element_type.32) | copy-start | bytes 1179652
  526.3 42.6 %collective-permute-start.2 = (bf16[3072,512]{1,0:T(8,128)(2,1)}, bf16[3072,512]{1,0:T(8,128)(2,1)S(1)}, u32[]{:S(2)}, u32[]{:S(2)}) collective-permute-start(bf16[3072,512]{1,0:T(8,128)(2,1)} %get-tuple-element.364), channel_id=1, source_target_pairs={{0,1},{1,2},{2,3},{3,4},{4,5},{5,6},{6,7},{7,0}} | collective-permute-start | bytes 9437192 | tf_op jit(solution)/shard_map/while/body/eval_jaxpr/ppermute | solution.py:22
  526.3 41.8 %collective-permute-start.3 = (bf16[3072,64]{0,1:T(8,128)(2,1)}, bf16[3072,64]{0,1:T(8,128)(2,1)S(1)}, u32[]{:S(2)}, u32[]{:S(2)}) collective-permute-start(bf16[3072,64]{0,1:T(8,128)(2,1)} %get-tuple-element.365), channel_id=1, source_target_pairs={{0,1},{1,2},{2,3},{3,4},{4,5},{5,6},{6,7},{7,0}} | collective-permute-start | bytes 1179656 | tf_op jit(solution)/shard_map/while/body/eval_jaxpr/ppermute | solution.py:23
  593.0 42.6 %collective-permute-start.2 = (bf16[3072,512]{1,0:T(8,128)(2,1)}, bf16[3072,512]{1,0:T(8,128)(2,1)S(1)}, u32[]{:S(2)}, u32[]{:S(2)}) collective-permute-start(bf16[3072,512]{1,0:T(8,128)(2,1)} %get-tuple-element.364), channel_id=1, source_target_pairs={{0,1},{1,2},{2,3},{3,4},{4,5},{5,6},{6,7},{7,0}} | collective-permute-start | bytes 9437192 | tf_op jit(solution)/shard_map/while/body/eval_jaxpr/ppermute | solution.py:22
  593.0 41.8 %collective-permute-start.3 = (bf16[3072,64]{0,1:T(8,128)(2,1)}, bf16[3072,64]{0,1:T(8,128)(2,1)S(1)}, u32[]{:S(2)}, u32[]{:S(2)}) collective-permute-start(bf16[3072,64]{0,1:T(8,128)(2,1)} %get-tuple-element.365), channel_id=1, source_target_pairs={{0,1},{1,2},{2,3},{3,4},{4,5},{5,6},{6,7},{7,0}} | collective-permute-start | bytes 1179656 | tf_op jit(solution)/shard_map/while/body/eval_jaxpr/ppermute | solution.py:23
  659.7 42.6 %collective-permute-start.2 = (bf16[3072,512]{1,0:T(8,128)(2,1)}, bf16[3072,512]{1,0:T(8,128)(2,1)S(1)}, u32[]{:S(2)}, u32[]{:S(2)}) collective-permute-start(bf16[3072,512]{1,0:T(8,128)(2,1)} %get-tuple-element.364), channel_id=1, source_target_pairs={{0,1},{1,2},{2,3},{3,4},{4,5},{5,6},{6,7},{7,0}} | collective-permute-start | bytes 9437192 | tf_op jit(solution)/shard_map/while/body/eval_jaxpr/ppermute | solution.py:22
  659.7 41.8 %collective-permute-start.3 = (bf16[3072,64]{0,1:T(8,128)(2,1)}, bf16[3072,64]{0,1:T(8,128)(2,1)S(1)}, u32[]{:S(2)}, u32[]{:S(2)}) collective-permute-start(bf16[3072,64]{0,1:T(8,128)(2,1)} %get-tuple-element.365), channel_id=1, source_target_pairs={{0,1},{1,2},{2,3},{3,4},{4,5},{5,6},{6,7},{7,0}} | collective-permute-start | bytes 1179656 | tf_op jit(solution)/shard_map/while/body/eval_jaxpr/ppermute | solution.py:23
  726.4 42.6 %collective-permute-start.2 = (bf16[3072,512]{1,0:T(8,128)(2,1)}, bf16[3072,512]{1,0:T(8,128)(2,1)S(1)}, u32[]{:S(2)}, u32[]{:S(2)}) collective-permute-start(bf16[3072,512]{1,0:T(8,128)(2,1)} %get-tuple-element.364), channel_id=1, source_target_pairs={{0,1},{1,2},{2,3},{3,4},{4,5},{5,6},{6,7},{7,0}} | collective-permute-start | bytes 9437192 | tf_op jit(solution)/shard_map/while/body/eval_jaxpr/ppermute | solution.py:22
  726.4 41.8 %collective-permute-start.3 = (bf16[3072,64]{0,1:T(8,128)(2,1)}, bf16[3072,64]{0,1:T(8,128)(2,1)S(1)}, u32[]{:S(2)}, u32[]{:S(2)}) collective-permute-start(bf16[3072,64]{0,1:T(8,128)(2,1)} %get-tuple-element.365), channel_id=1, source_target_pairs={{0,1},{1,2},{2,3},{3,4},{4,5},{5,6},{6,7},{7,0}} | collective-permute-start | bytes 1179656 | tf_op jit(solution)/shard_map/while/body/eval_jaxpr/ppermute | solution.py:23
  793.1 42.6 %collective-permute-start.2 = (bf16[3072,512]{1,0:T(8,128)(2,1)}, bf16[3072,512]{1,0:T(8,128)(2,1)S(1)}, u32[]{:S(2)}, u32[]{:S(2)}) collective-permute-start(bf16[3072,512]{1,0:T(8,128)(2,1)} %get-tuple-element.364), channel_id=1, source_target_pairs={{0,1},{1,2},{2,3},{3,4},{4,5},{5,6},{6,7},{7,0}} | collective-permute-start | bytes 9437192 | tf_op jit(solution)/shard_map/while/body/eval_jaxpr/ppermute | solution.py:22
  793.1 41.8 %collective-permute-start.3 = (bf16[3072,64]{0,1:T(8,128)(2,1)}, bf16[3072,64]{0,1:T(8,128)(2,1)S(1)}, u32[]{:S(2)}, u32[]{:S(2)}) collective-permute-start(bf16[3072,64]{0,1:T(8,128)(2,1)} %get-tuple-element.365), channel_id=1, source_target_pairs={{0,1},{1,2},{2,3},{3,4},{4,5},{5,6},{6,7},{7,0}} | collective-permute-start | bytes 1179656 | tf_op jit(solution)/shard_map/while/body/eval_jaxpr/ppermute | solution.py:23
  859.8 42.6 %collective-permute-start.2 = (bf16[3072,512]{1,0:T(8,128)(2,1)}, bf16[3072,512]{1,0:T(8,128)(2,1)S(1)}, u32[]{:S(2)}, u32[]{:S(2)}) collective-permute-start(bf16[3072,512]{1,0:T(8,128)(2,1)} %get-tuple-element.364), channel_id=1, source_target_pairs={{0,1},{1,2},{2,3},{3,4},{4,5},{5,6},{6,7},{7,0}} | collective-permute-start | bytes 9437192 | tf_op jit(solution)/shard_map/while/body/eval_jaxpr/ppermute | solution.py:22
  859.8 41.8 %collective-permute-start.3 = (bf16[3072,64]{0,1:T(8,128)(2,1)}, bf16[3072,64]{0,1:T(8,128)(2,1)S(1)}, u32[]{:S(2)}, u32[]{:S(2)}) collective-permute-start(bf16[3072,64]{0,1:T(8,128)(2,1)} %get-tuple-element.365), channel_id=1, source_target_pairs={{0,1},{1,2},{2,3},{3,4},{4,5},{5,6},{6,7},{7,0}} | collective-permute-start | bytes 1179656 | tf_op jit(solution)/shard_map/while/body/eval_jaxpr/ppermute | solution.py:23
  926.5 42.6 %collective-permute-start.2 = (bf16[3072,512]{1,0:T(8,128)(2,1)}, bf16[3072,512]{1,0:T(8,128)(2,1)S(1)}, u32[]{:S(2)}, u32[]{:S(2)}) collective-permute-start(bf16[3072,512]{1,0:T(8,128)(2,1)} %get-tuple-element.364), channel_id=1, source_target_pairs={{0,1},{1,2},{2,3},{3,4},{4,5},{5,6},{6,7},{7,0}} | collective-permute-start | bytes 9437192 | tf_op jit(solution)/shard_map/while/body/eval_jaxpr/ppermute | solution.py:22
  926.5 41.8 %collective-permute-start.3 = (bf16[3072,64]{0,1:T(8,128)(2,1)}, bf16[3072,64]{0,1:T(8,128)(2,1)S(1)}, u32[]{:S(2)}, u32[]{:S(2)}) collective-permute-start(bf16[3072,64]{0,1:T(8,128)(2,1)} %get-tuple-element.365), channel_id=1, source_target_pairs={{0,1},{1,2},{2,3},{3,4},{4,5},{5,6},{6,7},{7,0}} | collective-permute-start | bytes 1179656 | tf_op jit(solution)/shard_map/while/body/eval_jaxpr/ppermute | solution.py:23
where the time goes:
time: 994 us; the launch traced here: 993 us
  waiting for transfers between devices  581 us (58%)
  matrix products  343 us (35%)
  local copies, waits for them, and re-layouts  47.7 us (5%)
  other arithmetic  14.1 us (1%)
    ppermute x14, waiting for transfers between devices, visit_step(): v_vis = lax.ppermute(v_vis, 'row', shift_pairs)  581 us
    dot_general x16, matrix products, kernel_product(): return jnp.dot(kern_tile, v_cols, preferred_element_type=jnp.float32)  326 us
    while x28, local copies, waits for them, and re-layouts  34 us
  transfers between devices with their start and end apart: 28, of which 14 were waited for; matrix products, arithmetic and copies ran while one was open for 1% of the time, Pallas kernels for 0%

commit v1 on v0

v1 whole, which is shorter than its diff:
```python
import functools
import math

import jax
import jax.numpy as jnp
from jax import lax
from jax.experimental import pallas as pl
from jax.experimental.pallas import tpu as pltpu
from jax.sharding import PartitionSpec as P

MESH = pl.DeviceIdType.MESH
T = 256
FEAT = 512
COLS = 64
NCH = 12
NREL = 8
STEPS = NREL * NCH
PIECE = 64
NP = T // PIECE
NI = NCH // 2
RES_IN, RES_OF = 3, 8
N_RES = (STEPS - 24) // RES_OF * RES_IN
RING = 5
N_STREAM = STEPS - N_RES
XR = 3


def chunk_of(s):
    j = lax.rem(s + 2, 4)
    v = lax.div(s - 22, 4) - 1
    late = jnp.where(s < 26, 0, jnp.where(s >= 94, 1, lax.div(j, 2)))
    group = jnp.where(s < 26, 0, jnp.where(s >= 94, 17, v + 1 - late))
    side = lax.rem(s, 2)
    far = group >= 12
    rel = jnp.where(far, 6, 2 + 2 * side) + late
    chunk = jnp.where(far, 2 * (group - 12) + side, group)
    near_rel = lax.div(s, NCH)
    near_chunk = lax.rem(s, NCH)
    return jnp.where(s < 24, near_rel, rel), jnp.where(s < 24, near_chunk, chunk)


def stream_of(s):
    u = jnp.maximum(s - 24, 0)
    w = lax.rem(u, RES_OF)
    o = lax.div(u, RES_OF)
    streamed = jnp.logical_or(s < 24, w >= RES_IN)
    number = jnp.where(s < 24, s, 24 + o * (RES_OF - RES_IN) + w - RES_IN)
    slot = jnp.where(streamed, N_RES + lax.rem(number, RING), o * RES_IN + w)
    return streamed, number, slot


def body(
    x_hbm, vt_hbm, ls_ref, os_ref,
    out_ref, xall, kst,
    xt, vt, yall, kbuf, xr, nj, ni,
    ld_sem, kw_sem, kr_sem, vl_sem,
    rx_sem, rv_sem, so_x, so_v, sp_x, sp_v, sn_x, sn_v, ys_sem, yr_sem,
    ysum,
):
    me = lax.axis_index("row")
    partner = me + 1 - 2 * lax.rem(me, 2)
    nbr_x = me + 2 - 4 * lax.rem(lax.div(me, 2), 2)
    nbr_y = me + 4 - 8 * lax.div(me, 4)

    def remote(src, dst, ss, rs, dev):
        return pltpu.make_async_remote_copy(
            src_ref=src, dst_ref=dst, send_sem=ss, recv_sem=rs, device_id={"row": dev}, device_id_type=MESH
        )

    def send_own(k, which, dev):
        slot = (1, 2, 4)[which]
        return (
            remote(x_hbm.at[k], xall.at[slot, k], so_x.at[which, k], rx_sem.at[slot, k], dev),
            remote(vt_hbm.at[k], vt.at[slot, k], so_v.at[which, k], rv_sem.at[slot, k], dev),
        )

    def forward_partner(rel, k):
        row = lax.div(rel, 2) - 1
        return (
            remote(xall.at[rel, k], xall.at[rel + 1, k], sp_x.at[row, k], rx_sem.at[rel + 1, k], partner),
            remote(vt.at[rel, k], vt.at[rel + 1, k], sp_v.at[row, k], rv_sem.at[rel + 1, k], partner),
        )

    def forward_nbr(rel, k, dev):
        return (
            remote(xall.at[rel, k], xall.at[6, k], sn_x.at[k], rx_sem.at[6, k], dev),
            remote(vt.at[rel, k], vt.at[6, k], sn_v.at[k], rv_sem.at[6, k], dev),
        )

    barrier = pltpu.get_barrier_semaphore()
    for dev in (partner, nbr_x, nbr_y):
        pl.semaphore_signal(barrier, inc=1, device_id={"row": dev}, device_id_type=MESH)

    own_v = pltpu.make_async_copy(vt_hbm, vt.at[0], vl_sem)
    own_v.start()

    def load_own(k, slot):
        return pltpu.make_async_copy(x_hbm.at[k], xr.at[slot], ld_sem.at[slot])

    load_own(0, 0).start()
    pl.semaphore_wait(barrier, 3)

    @pl.loop(0, NCH)
    def _(k):
        for which, dev in enumerate((partner, nbr_x, nbr_y)):
            for copy in send_own(k, which, dev):
                copy.start()

    load_own(1, 1).start()

    @pl.loop(0, NCH)
    def _(k):
        slot = lax.rem(k, 2)
        load_own(k, slot).wait()
        norm = jnp.zeros((1, T), jnp.float32)
        for h in range(2):
            part = xr[slot, :, h * T : (h + 1) * T].astype(jnp.float32).T
            norm = norm + jnp.sum(part * part, axis=0, keepdims=True)
            xt[k, h * T : (h + 1) * T, :] = (part * -2.0).astype(jnp.bfloat16)
        ni[k] = jnp.broadcast_to(norm, (8, T))

        @pl.when(k + 2 < NCH)
        def _():
            load_own(k + 2, slot).start()

    own_v.wait()
    load_own(0, 0).start()

    scale = jnp.full((1, T), ls_ref[0], jnp.float32)
    rate = -math.log2(math.e) / (2.0 * scale * scale)
    amp = jnp.full((1, T), os_ref[0], jnp.float32)

    @pl.loop(0, NCH)
    def _(k):
        ysum[k] = jnp.zeros((COLS, T), jnp.float32)

    def write_k(number):
        slot = lax.rem(number, RING)
        return pltpu.make_async_copy(kbuf.at[N_RES + slot], kst.at[number], kw_sem.at[slot])

    def read_k(number):
        slot = lax.rem(number, RING)
        return pltpu.make_async_copy(kst.at[number], kbuf.at[N_RES + slot], kr_sem.at[slot])

    def tile(x_slot, k_slot, n_slot, i):
        gram_tile = jnp.dot(
            xr[x_slot], xt[i], preferred_element_type=jnp.float32
        )
        dist = jnp.maximum((nj[n_slot] + ni[i, 0:1, :]) + gram_tile, 0.0)
        kbuf[k_slot, i] = (amp * jnp.exp2(dist * rate)).astype(jnp.bfloat16)

    def apply(k_slot, lhs, i):
        ysum[i] += jnp.dot(lhs, kbuf[k_slot, i], preferred_element_type=jnp.float32)

    def fetch(s):
        rel, k = chunk_of(s)
        slot = lax.rem(s, XR)

        @pl.when(rel == 0)
        def _():
            load_own(k, slot).start()

        @pl.when(rel > 0)
        def _():
            remote(xall.at[rel, k], xall.at[rel, k], so_x.at[0, 0], rx_sem.at[rel, k], partner).wait_recv()
            remote(vt.at[rel, k], vt.at[rel, k], so_v.at[0, 0], rv_sem.at[rel, k], partner).wait_recv()
            pltpu.make_async_copy(xall.at[rel, k], xr.at[slot], ld_sem.at[slot]).start()

        @pl.when(jnp.logical_and(rel >= 2, lax.rem(rel, 2) == 0))
        def _():
            for copy in forward_partner(rel, k):
                copy.start()

        @pl.when(jnp.logical_and(rel == 2, lax.rem(k, 2) == 1))
        def _():
            for copy in forward_nbr(2, k, nbr_y):
                copy.start()

        @pl.when(jnp.logical_and(rel == 4, lax.rem(k, 2) == 0))
        def _():
            for copy in forward_nbr(4, k, nbr_x):
                copy.start()

    def trip(s, first):
        if first:
            fetch(jnp.int32(1))
        else:

            @pl.when(s + 1 < STEPS)
            def _():
                fetch(s + 1)

            done, number, _ = stream_of(s - 2)

            @pl.when(jnp.logical_and(done, s >= 2))
            def _():
                write_k(number).start()

        streamed, number, k_slot = stream_of(s)

        @pl.when(jnp.logical_and(streamed, number >= RING))
        def _():
            write_k(number - RING).wait()

        x_slot = lax.rem(s, XR)
        n_slot = lax.rem(s, 2)
        load_own(0, x_slot).wait()
        rel, k = chunk_of(s)
        for p in range(NP):
            rows = slice(p * PIECE, (p + 1) * PIECE)
            part = xr[x_slot, rows, :].astype(jnp.float32)
            norm = jnp.sum(part * part, axis=1, keepdims=True)
            nj[n_slot, rows, :] = jnp.broadcast_to(norm, (PIECE, T))
        for i in range(NCH):
            tile(x_slot, k_slot, n_slot, i)
            if i >= 1:
                apply(k_slot, vt[rel, k], i - 1)
        apply(k_slot, vt[rel, k], NCH - 1)

    trip(jnp.int32(0), True)

    @pl.loop(1, STEPS)
    def _(s):
        trip(s, False)

    @pl.loop(0, NCH)
    def _(k):
        yall[0, k] = ysum[k].astype(jnp.bfloat16)
        ysum[k] = jnp.zeros((COLS, T), jnp.float32)

    for back in (2, 1):
        streamed, number, _ = stream_of(jnp.int32(STEPS - back))

        @pl.when(streamed)
        def _():
            write_k(number).start()

    @pl.loop(0, NCH)
    def _(k):
        for which, dev in enumerate((partner, nbr_x, nbr_y)):
            for copy in send_own(k, which, dev):
                copy.wait_send()
        for rel in (2, 4, 6):
            for copy in forward_partner(rel, k):
                copy.wait_send()
        for copy in forward_nbr(2, k, nbr_y):
            copy.wait_send()

    half = NCH // 2

    def y_copy(src_rel, dst_rel, lo, n, idx, dev):
        return remote(
            yall.at[src_rel, pl.ds(lo, n)], yall.at[dst_rel, pl.ds(lo, n)], ys_sem.at[idx], yr_sem.at[idx], dev
        )

    y_moves = (
        (0, 1, 0, NCH, partner),
        (0, 2, 0, NCH, nbr_x),
        (0, 4, 0, NCH, nbr_y),
        (2, 3, 0, NCH, partner),
        (4, 5, 0, NCH, partner),
        (4, 6, 0, half, nbr_x),
        (2, 6, half, half, nbr_y),
        (6, 7, 0, NCH, partner),
    )

    def y_move(idx):
        src, dst, lo, n, dev = y_moves[idx]
        return y_copy(src, dst, lo, n, idx, dev)

    def y_arrived(idx):
        _, dst, lo, n, dev = y_moves[idx]
        return y_copy(dst, dst, lo, n, idx, dev)

    for idx in range(3):
        y_move(idx).start()

    for back in range(RING):
        write_k(jnp.int32(N_STREAM - RING + back)).wait()
    for number in range(RING):
        read_k(jnp.int32(number)).start()

    def second(s):
        @pl.when(s == 12)
        def _():
            y_arrived(0).wait_recv()

        @pl.when(s == 20)
        def _():
            y_arrived(1).wait_recv()
            y_arrived(2).wait_recv()
            for idx in range(3, 7):
                y_move(idx).start()

        @pl.when(s == 28)
        def _():
            y_arrived(3).wait_recv()
            y_arrived(4).wait_recv()

        @pl.when(s == 56)
        def _():
            y_arrived(5).wait_recv()
            y_arrived(6).wait_recv()
            y_move(7).start()

        @pl.when(s == 70)
        def _():
            y_arrived(7).wait_recv()

        streamed, number, slot = stream_of(s)

        @pl.when(streamed)
        def _():
            read_k(number).wait()

        rel, k = chunk_of(s)
        for i in range(NCH):
            apply(slot, yall[rel, k], i)

        @pl.when(jnp.logical_and(streamed, number + RING < N_STREAM))
        def _():
            read_k(number + RING).start()

    @pl.loop(0, STEPS)
    def _(s):
        second(s)

    for idx in range(8):
        y_move(idx).wait_send()

    @pl.loop(0, NCH)
    def _(k):
        out_ref[k] = ysum[k]


def solution(mesh):
    rows = NCH * T

    def local_program(x_loc, v_loc, length_scale, out_scale):
        vt_loc = v_loc.reshape(NCH, T, COLS).transpose(0, 2, 1)
        dma = pltpu.SemaphoreType.DMA
        out, _, _ = pl.pallas_call(
            body,
            out_shape=(
                jax.ShapeDtypeStruct((NCH, COLS, T), jnp.float32),
                jax.ShapeDtypeStruct((NREL, NCH, T, FEAT), jnp.bfloat16),
                jax.ShapeDtypeStruct((N_STREAM, NCH, T, T), jnp.bfloat16),
            ),
            in_specs=[
                pl.BlockSpec(memory_space=pltpu.HBM),
                pl.BlockSpec(memory_space=pltpu.HBM),
                pl.BlockSpec(memory_space=pltpu.SMEM),
                pl.BlockSpec(memory_space=pltpu.SMEM),
            ],
            out_specs=(
                pl.BlockSpec(memory_space=pltpu.VMEM),
                pl.BlockSpec(memory_space=pltpu.HBM),
                pl.BlockSpec(memory_space=pltpu.HBM),
            ),
            scratch_shapes=[
                pltpu.VMEM((NCH, FEAT, T), jnp.bfloat16),
                pltpu.VMEM((NREL, NCH, COLS, T), jnp.bfloat16),
                pltpu.VMEM((NREL, NCH, COLS, T), jnp.bfloat16),
                pltpu.VMEM((N_RES + RING, NCH, T, T), jnp.bfloat16),
                pltpu.VMEM((XR, T, FEAT), jnp.bfloat16),
                pltpu.VMEM((2, T, T), jnp.float32),
                pltpu.VMEM((NCH, 8, T), jnp.float32),
                dma((XR,)), dma((RING,)), dma((RING,)), dma,
                dma((NREL, NCH)), dma((NREL, NCH)),
                dma((3, NCH)), dma((3, NCH)),
                dma((3, NCH)), dma((3, NCH)),
                dma((NCH,)), dma((NCH,)),
                dma((8,)), dma((8,)),
                pltpu.VMEM((NCH, COLS, T), jnp.float32),
            ],
            compiler_params=pltpu.CompilerParams(
                collective_id=0, has_side_effects=True, vmem_limit_bytes=67_043_328
            ),
        )(x_loc.reshape(NCH, T, FEAT), vt_loc, length_scale, out_scale)
        return out.transpose(0, 2, 1).reshape(rows, COLS)

    row_spec = P(("task", "row"), None)
    return jax.shard_map(
        local_program,
        mesh=mesh,
        in_specs=(row_spec, row_spec, P("task"), P("task")),
        out_specs=row_spec,
        check_vma=False,
    )
```

time: 994 us -> 275 us (0.28)
  waiting for transfers between devices: 581 us -> 0 us
  matrix products: 343 us -> 0 us
  Pallas kernels: 0 us -> 270 us
  local copies, waits for them, and re-layouts: 47.7 us -> 3.86 us
  other arithmetic: 14.1 us -> 0 us
    ppermute x28 -> x0, waiting for transfers between devices: 581 us -> none  [the longest x14 581 us: visit_step(): v_vis = lax.ppermute(v_vis, 'row', shift_pairs)]
    dot_general x17 -> x0, matrix products: 343 us -> none  [the longest x16 326 us: kernel_product(): return jnp.dot(kern_tile, v_cols, preferred_element_type=jnp.float32)]
    pallas_call x0 -> x1, Pallas kernels: none -> 270 us  [local_program(): pl.pallas_call(body, out_shape=(jax.ShapeDtypeStruct((NCH, COLS, T), jnp....]
    while x28 -> x0, local copies, waits for them, and re-layouts: 34 us -> none
    unnamed x9 -> x0, local copies, waits for them, and re-layouts: 13.7 us -> none
    reduce_sum x15 -> x0, other arithmetic: 12.8 us -> none  [the longest x14 9.62 us: visit_step(): norm_vis = jnp.sum(jnp.square(x_vis.astype(jnp.float32)), axis=1)]
  transfers between devices with their start and end apart: 28 -> 0, of which waited for: 14 -> 0; matrix products, arithmetic and copies ran while one was open for 1% -> 0% of each run, Pallas kernels for 0% -> 0%
where the time goes in v1:
time: 275 us
  Pallas kernels  270 us (98%)
  local copies, waits for them, and re-layouts  3.86 us (1%)
    pallas_call x1, Pallas kernels, local_program(): pl.pallas_call(body, out_shape=(jax.ShapeDtypeStruct((NCH, COLS, T), jnp....  270 us

profile of v1, /device:TPU:0, one launch (start us, length us, event | category | flops | bytes accessed | tf_op | source)
XLA Modules:
  0.0 274.9 jit_solution(4511664116428519637)
XLA Ops:
  1.3 1.8 copy.10
  3.1 269.7 %shard_map.46 = (f32[12,64,256]{2,1,0:T(8,128)}, bf16[8,12,256,512]{3,2,1,0:T(8,128)(2,1)}, bf16[69,12,256,256]{3,2,1,0:T(8,128)(2,1)}) custom-call(bf16[12,256,512]{2,1,0:T(8,128)(2,1)} %bitcast.11, bf16[12,64,256]{2,1,0:T(8,128)(2,1)} %bitcast.12, f32[1]{0:T(128)S(6)} %copy.11.ls_ref, f32[1]{0:T(128)S(6)} %copy.12.os_ref), custom_call_target="tpu_custom_call" | custom-call | tf_op jit(solution)/shard_map/pallas_call | solution.py:342
  272.8 2.1 copy.8

commit v2 on v1

--- a/solution.py
+++ b/solution.py
@@ -142,10 +142,10 @@
         slot = lax.rem(number, RING)
         return pltpu.make_async_copy(kst.at[number], kbuf.at[N_RES + slot], kr_sem.at[slot])
 
-    def tile(x_slot, k_slot, n_slot, i):
-        gram_tile = jnp.dot(
-            xr[x_slot], xt[i], preferred_element_type=jnp.float32
-        )
+    def gram(x_slot, i):
+        return jnp.dot(xr[x_slot], xt[i], preferred_element_type=jnp.float32)
+
+    def weigh(gram_tile, k_slot, n_slot, i):
         dist = jnp.maximum((nj[n_slot] + ni[i, 0:1, :]) + gram_tile, 0.0)
         kbuf[k_slot, i] = (amp * jnp.exp2(dist * rate)).astype(jnp.bfloat16)
 
@@ -212,10 +212,9 @@
             norm = jnp.sum(part * part, axis=1, keepdims=True)
             nj[n_slot, rows, :] = jnp.broadcast_to(norm, (PIECE, T))
         for i in range(NCH):
-            tile(x_slot, k_slot, n_slot, i)
-            if i >= 1:
-                apply(k_slot, vt[rel, k], i - 1)
-        apply(k_slot, vt[rel, k], NCH - 1)
+            weigh(gram(x_slot, i), k_slot, n_slot, i)
+        for i in range(NCH):
+            apply(k_slot, vt[rel, k], i)
 
     trip(jnp.int32(0), True)
 

time: 275 us -> 198 us (0.72)
  Pallas kernels: 270 us -> 192 us
    pallas_call x1, Pallas kernels: 270 us -> 192 us  [local_program(): pl.pallas_call(body, out_shape=(jax.ShapeDtypeStruct((NCH, COLS, T), jnp....]
where the time goes in v2:
time: 198 us; the launch traced here: 197 us
  Pallas kernels  192 us (97%)
  local copies, waits for them, and re-layouts  3.86 us (2%)
    pallas_call x1, Pallas kernels, local_program(): pl.pallas_call(body, out_shape=(jax.ShapeDtypeStruct((NCH, COLS, T), jnp....  192 us

profile of v2, /device:TPU:0, one launch (start us, length us, event | category | flops | bytes accessed | tf_op | source)
XLA Modules:
  0.0 197.3 jit_solution(5824039909331135926)
XLA Ops:
  1.3 1.8 copy.10
  3.1 192.2 %shard_map.46 = (f32[12,64,256]{2,1,0:T(8,128)}, bf16[8,12,256,512]{3,2,1,0:T(8,128)(2,1)}, bf16[69,12,256,256]{3,2,1,0:T(8,128)(2,1)}) custom-call(bf16[12,256,512]{2,1,0:T(8,128)(2,1)} %bitcast.11, bf16[12,64,256]{2,1,0:T(8,128)(2,1)} %bitcast.12, f32[1]{0:T(128)S(6)} %copy.11.ls_ref, f32[1]{0:T(128)S(6)} %copy.12.os_ref), custom_call_target="tpu_custom_call" | custom-call | tf_op jit(solution)/shard_map/pallas_call | solution.py:341
  195.2 2.1 %copy.8 = f32[12,8,8,256]{3,2,0,1:T(8,128)} copy(f32[12,8,8,256]{3,2,1,0:T(8,128)} %bitcast.13) | data formatting | bytes 1572864 | tf_op jit(solution)/shard_map/reshape | solution.py:379

commit v3 on v2

--- a/solution.py
+++ b/solution.py
@@ -18,11 +18,12 @@
 PIECE = 64
 NP = T // PIECE
 NI = NCH // 2
-RES_IN, RES_OF = 3, 8
-N_RES = (STEPS - 24) // RES_OF * RES_IN
-RING = 5
-N_STREAM = STEPS - N_RES
-XR = 3
+PAIRS = STEPS // 2
+RES_IN, RES_OF = 2, 5
+N_RES = (PAIRS - 12) // RES_OF * RES_IN
+RING = 3
+N_STREAM = PAIRS - N_RES
+XR = 2
 
 
 def chunk_of(s):
@@ -39,20 +40,20 @@
     return jnp.where(s < 24, near_rel, rel), jnp.where(s < 24, near_chunk, chunk)
 
 
-def stream_of(s):
-    u = jnp.maximum(s - 24, 0)
+def stream_of(t):
+    u = jnp.maximum(t - 12, 0)
     w = lax.rem(u, RES_OF)
     o = lax.div(u, RES_OF)
-    streamed = jnp.logical_or(s < 24, w >= RES_IN)
-    number = jnp.where(s < 24, s, 24 + o * (RES_OF - RES_IN) + w - RES_IN)
-    slot = jnp.where(streamed, N_RES + lax.rem(number, RING), o * RES_IN + w)
-    return streamed, number, slot
+    keep = jnp.where(o == (PAIRS - 12) // RES_OF, 0, RES_IN)
+    streamed = jnp.logical_or(t < 12, w >= keep)
+    number = jnp.where(t < 12, t, 12 + o * (RES_OF - RES_IN) + w - keep)
+    return streamed, number, o * RES_IN + w
 
 
 def body(
     x_hbm, vt_hbm, ls_ref, os_ref,
     out_ref, xall, kst,
-    xt, vt, yall, kbuf, xr, nj, ni,
+    xt, vt, yall, kept, stage, xr, nj, ni,
     ld_sem, kw_sem, kr_sem, vl_sem,
     rx_sem, rv_sem, so_x, so_v, sp_x, sp_v, sn_x, sn_v, ys_sem, yr_sem,
     ysum,
@@ -94,10 +95,10 @@
     own_v = pltpu.make_async_copy(vt_hbm, vt.at[0], vl_sem)
     own_v.start()
 
-    def load_own(k, slot):
-        return pltpu.make_async_copy(x_hbm.at[k], xr.at[slot], ld_sem.at[slot])
-
-    load_own(0, 0).start()
+    def load_own(k, slot, half):
+        return pltpu.make_async_copy(x_hbm.at[k], xr.at[slot, pl.ds(half * T, T)], ld_sem.at[slot, half])
+
+    load_own(0, 0, 0).start()
     pl.semaphore_wait(barrier, 3)
 
     @pl.loop(0, NCH)
@@ -106,65 +107,84 @@
             for copy in send_own(k, which, dev):
                 copy.start()
 
-    load_own(1, 1).start()
+    load_own(1, 1, 0).start()
 
     @pl.loop(0, NCH)
     def _(k):
         slot = lax.rem(k, 2)
-        load_own(k, slot).wait()
+        load_own(k, slot, 0).wait()
         norm = jnp.zeros((1, T), jnp.float32)
         for h in range(2):
-            part = xr[slot, :, h * T : (h + 1) * T].astype(jnp.float32).T
+            part = xr[slot, :T, h * T : (h + 1) * T].astype(jnp.float32).T
             norm = norm + jnp.sum(part * part, axis=0, keepdims=True)
             xt[k, h * T : (h + 1) * T, :] = (part * -2.0).astype(jnp.bfloat16)
         ni[k] = jnp.broadcast_to(norm, (8, T))
 
         @pl.when(k + 2 < NCH)
         def _():
-            load_own(k + 2, slot).start()
+            load_own(k + 2, slot, 0).start()
 
     own_v.wait()
-    load_own(0, 0).start()
-
-    scale = jnp.full((1, T), ls_ref[0], jnp.float32)
+    load_own(0, 0, 0).start()
+    load_own(1, 0, 1).start()
+
+    scale = jnp.full((1, 128), ls_ref[0], jnp.float32)
     rate = -math.log2(math.e) / (2.0 * scale * scale)
-    amp = jnp.full((1, T), os_ref[0], jnp.float32)
+    amp = jnp.full((1, 128), os_ref[0], jnp.float32)
 
     @pl.loop(0, NCH)
     def _(k):
         ysum[k] = jnp.zeros((COLS, T), jnp.float32)
 
-    def write_k(number):
-        slot = lax.rem(number, RING)
-        return pltpu.make_async_copy(kbuf.at[N_RES + slot], kst.at[number], kw_sem.at[slot])
+    def write_k(t, parity):
+        streamed, number, slot = stream_of(t)
+
+        @pl.when(streamed)
+        def _():
+            pltpu.make_async_copy(stage.at[parity], kst.at[number], kw_sem.at[parity]).start()
+
+        @pl.when(jnp.logical_not(streamed))
+        def _():
+            pltpu.make_async_copy(stage.at[parity], kept.at[slot], kw_sem.at[parity]).start()
+
+    def written(parity):
+        pltpu.make_async_copy(stage.at[parity], kst.at[0], kw_sem.at[parity]).wait()
 
     def read_k(number):
         slot = lax.rem(number, RING)
-        return pltpu.make_async_copy(kst.at[number], kbuf.at[N_RES + slot], kr_sem.at[slot])
-
-    def gram(x_slot, i):
-        return jnp.dot(xr[x_slot], xt[i], preferred_element_type=jnp.float32)
-
-    def weigh(gram_tile, k_slot, n_slot, i):
-        dist = jnp.maximum((nj[n_slot] + ni[i, 0:1, :]) + gram_tile, 0.0)
-        kbuf[k_slot, i] = (amp * jnp.exp2(dist * rate)).astype(jnp.bfloat16)
-
-    def apply(k_slot, lhs, i):
-        ysum[i] += jnp.dot(lhs, kbuf[k_slot, i], preferred_element_type=jnp.float32)
+        return pltpu.make_async_copy(kst.at[number], stage.at[slot], kr_sem.at[slot])
+
+    def weigh(x_slot, parity, i):
+        gram_tile = jnp.dot(xr[x_slot], xt[i], preferred_element_type=jnp.float32)
+        for h in range(2):
+            lanes = slice(h * 128, (h + 1) * 128)
+            dist = jnp.maximum((nj[...] + ni[i, 0:1, lanes]) + gram_tile[:, lanes], 0.0)
+            stage[parity, i, :, lanes] = (amp * jnp.exp2(dist * rate)).astype(jnp.bfloat16)
+
+    def apply(source, slot, lhs, i):
+        ysum[i] += jnp.dot(lhs, source[slot, i], preferred_element_type=jnp.float32)
+
+    def pair_of(table, t):
+        rel, k = chunk_of(2 * t)
+        rel_2, k_2 = chunk_of(2 * t + 1)
+        return jnp.concatenate([table[rel, k], table[rel_2, k_2]], axis=1)
 
     def fetch(s):
         rel, k = chunk_of(s)
-        slot = lax.rem(s, XR)
+        half = lax.rem(s, 2)
+        slot = lax.rem(lax.div(s, 2), XR)
 
         @pl.when(rel == 0)
         def _():
-            load_own(k, slot).start()
+            load_own(k, slot, half).start()
 
         @pl.when(rel > 0)
         def _():
             remote(xall.at[rel, k], xall.at[rel, k], so_x.at[0, 0], rx_sem.at[rel, k], partner).wait_recv()
             remote(vt.at[rel, k], vt.at[rel, k], so_v.at[0, 0], rv_sem.at[rel, k], partner).wait_recv()
-            pltpu.make_async_copy(xall.at[rel, k], xr.at[slot], ld_sem.at[slot]).start()
+            pltpu.make_async_copy(
+                xall.at[rel, k], xr.at[slot, pl.ds(half * T, T)], ld_sem.at[slot, half]
+            ).start()
 
         @pl.when(jnp.logical_and(rel >= 2, lax.rem(rel, 2) == 0))
         def _():
@@ -181,58 +201,49 @@
             for copy in forward_nbr(4, k, nbr_x):
                 copy.start()
 
-    def trip(s, first):
-        if first:
-            fetch(jnp.int32(1))
-        else:
-
-            @pl.when(s + 1 < STEPS)
+    def trip(t, parity, place):
+        if place < 2:
+            fetch(2 * t + 2)
+            fetch(2 * t + 3)
+        if place > 0:
+            write_k(t - 1, 1 - parity)
+
+            @pl.when(t >= 2)
             def _():
-                fetch(s + 1)
-
-            done, number, _ = stream_of(s - 2)
-
-            @pl.when(jnp.logical_and(done, s >= 2))
-            def _():
-                write_k(number).start()
-
-        streamed, number, k_slot = stream_of(s)
-
-        @pl.when(jnp.logical_and(streamed, number >= RING))
-        def _():
-            write_k(number - RING).wait()
-
-        x_slot = lax.rem(s, XR)
-        n_slot = lax.rem(s, 2)
-        load_own(0, x_slot).wait()
-        rel, k = chunk_of(s)
-        for p in range(NP):
+                written(parity)
+
+        x_slot = parity
+        load_own(0, x_slot, 0).wait()
+        load_own(0, x_slot, 1).wait()
+        for p in range(2 * NP):
             rows = slice(p * PIECE, (p + 1) * PIECE)
             part = xr[x_slot, rows, :].astype(jnp.float32)
             norm = jnp.sum(part * part, axis=1, keepdims=True)
-            nj[n_slot, rows, :] = jnp.broadcast_to(norm, (PIECE, T))
+            nj[rows, :] = jnp.broadcast_to(norm, (PIECE, 128))
+        if place > 0:
+            lhs = pair_of(vt, t - 1)
         for i in range(NCH):
-            weigh(gram(x_slot, i), k_slot, n_slot, i)
-        for i in range(NCH):
-            apply(k_slot, vt[rel, k], i)
-
-    trip(jnp.int32(0), True)
-
-    @pl.loop(1, STEPS)
-    def _(s):
-        trip(s, False)
+            if place > 0:
+                apply(stage, 1 - parity, lhs, i)
+            weigh(x_slot, parity, i)
+
+    trip(jnp.int32(0), 0, 0)
+
+    @pl.loop(0, PAIRS // 2 - 1)
+    def _(m):
+        trip(2 * m + 1, 1, 1)
+        trip(2 * m + 2, 0, 1)
+
+    trip(jnp.int32(PAIRS - 1), 1, 2)
+    write_k(jnp.int32(PAIRS - 1), 1)
+    lhs = pair_of(vt, jnp.int32(PAIRS - 1))
+    for i in range(NCH):
+        apply(stage, 1, lhs, i)
 
     @pl.loop(0, NCH)
     def _(k):
         yall[0, k] = ysum[k].astype(jnp.bfloat16)
         ysum[k] = jnp.zeros((COLS, T), jnp.float32)
-
-    for back in (2, 1):
-        streamed, number, _ = stream_of(jnp.int32(STEPS - back))
-
-        @pl.when(streamed)
-        def _():
-            write_k(number).start()
 
     @pl.loop(0, NCH)
     def _(k):
@@ -274,12 +285,14 @@
     for idx in range(3):
         y_move(idx).start()
 
-    for back in range(RING):
-        write_k(jnp.int32(N_STREAM - RING + back)).wait()
+    for parity in range(2):
+        written(parity)
     for number in range(RING):
         read_k(jnp.int32(number)).start()
 
-    def second(s):
+    def second(t):
+        s = 2 * t
+
         @pl.when(s == 12)
         def _():
             y_arrived(0).wait_recv()
@@ -306,23 +319,31 @@
         def _():
             y_arrived(7).wait_recv()
 
-        streamed, number, slot = stream_of(s)
+        streamed, number, slot = stream_of(t)
 
         @pl.when(streamed)
         def _():
             read_k(number).wait()
 
-        rel, k = chunk_of(s)
-        for i in range(NCH):
-            apply(slot, yall[rel, k], i)
+        lhs = pair_of(yall, t)
+
+        @pl.when(streamed)
+        def _():
+            for i in range(NCH):
+                apply(stage, lax.rem(number, RING), lhs, i)
+
+        @pl.when(jnp.logical_not(streamed))
+        def _():
+            for i in range(NCH):
+                apply(kept, slot, lhs, i)
 
         @pl.when(jnp.logical_and(streamed, number + RING < N_STREAM))
         def _():
             read_k(number + RING).start()
 
-    @pl.loop(0, STEPS)
-    def _(s):
-        second(s)
+    @pl.loop(0, PAIRS)
+    def _(t):
+        second(t)
 
     for idx in range(8):
         y_move(idx).wait_send()
@@ -343,7 +364,7 @@
             out_shape=(
                 jax.ShapeDtypeStruct((NCH, COLS, T), jnp.float32),
                 jax.ShapeDtypeStruct((NREL, NCH, T, FEAT), jnp.bfloat16),
-                jax.ShapeDtypeStruct((N_STREAM, NCH, T, T), jnp.bfloat16),
+                jax.ShapeDtypeStruct((N_STREAM, NCH, 2 * T, T), jnp.bfloat16),
             ),
             in_specs=[
                 pl.BlockSpec(memory_space=pltpu.HBM),
@@ -360,11 +381,12 @@
                 pltpu.VMEM((NCH, FEAT, T), jnp.bfloat16),
                 pltpu.VMEM((NREL, NCH, COLS, T), jnp.bfloat16),
                 pltpu.VMEM((NREL, NCH, COLS, T), jnp.bfloat16),
-                pltpu.VMEM((N_RES + RING, NCH, T, T), jnp.bfloat16),
-                pltpu.VMEM((XR, T, FEAT), jnp.bfloat16),
-                pltpu.VMEM((2, T, T), jnp.float32),
+                pltpu.VMEM((N_RES, NCH, 2 * T, T), jnp.bfloat16),
+                pltpu.VMEM((RING, NCH, 2 * T, T), jnp.bfloat16),
+                pltpu.VMEM((XR, 2 * T, FEAT), jnp.bfloat16),
+                pltpu.VMEM((2 * T, 128), jnp.float32),
                 pltpu.VMEM((NCH, 8, T), jnp.float32),
-                dma((XR,)), dma((RING,)), dma((RING,)), dma,
+                dma((XR, 2)), dma((2,)), dma((RING,)), dma,
                 dma((NREL, NCH)), dma((NREL, NCH)),
                 dma((3, NCH)), dma((3, NCH)),
                 dma((3, NCH)), dma((3, NCH)),

time: 198 us -> 189 us (0.955)
  Pallas kernels: 192 us -> 184 us
    pallas_call x1, Pallas kernels: 192 us -> 184 us  [local_program(): pl.pallas_call(body, out_shape=(jax.ShapeDtypeStruct((NCH, COLS, T), jnp....]
where the time goes in v3:
time: 189 us
  Pallas kernels  184 us (97%)
  local copies, waits for them, and re-layouts  3.86 us (2%)
    pallas_call x1, Pallas kernels, local_program(): pl.pallas_call(body, out_shape=(jax.ShapeDtypeStruct((NCH, COLS, T), jnp....  184 us

profile of v3, /device:TPU:0, one launch (start us, length us, event | category | flops | bytes accessed | tf_op | source)
XLA Modules:
  0.0 189.0 jit_solution(15607068639162338897)
XLA Ops:
  1.3 1.8 copy.10
  3.1 183.8 %shard_map.46 = (f32[12,64,256]{2,1,0:T(8,128)}, bf16[8,12,256,512]{3,2,1,0:T(8,128)(2,1)}, bf16[34,12,512,256]{3,2,1,0:T(8,128)(2,1)}) custom-call(bf16[12,256,512]{2,1,0:T(8,128)(2,1)} %bitcast.11, bf16[12,64,256]{2,1,0:T(8,128)(2,1)} %bitcast.12, f32[1]{0:T(128)S(6)} %copy.11.ls_ref, f32[1]{0:T(128)S(6)} %copy.12.os_ref), custom_call_target="tpu_custom_call" | custom-call | tf_op jit(solution)/shard_map/pallas_call | solution.py:362
  186.9 2.1 %copy.8 = f32[12,8,8,256]{3,2,0,1:T(8,128)} copy(f32[12,8,8,256]{3,2,1,0:T(8,128)} %bitcast.13) | data formatting | bytes 1572864 | tf_op jit(solution)/shard_map/reshape | solution.py:401
